TPU v7x, 256 devices: a 8x8x2 block of a 8x8x16 slice. The times are simulated.
256 devices in a mesh: ga: 2 (over z), ta: 16 (over y, core), gy: 8 (over x).
Axes of the slice: x: 8, y: 8, z: 2, core: 2. Of those that a mesh axis runs over, the one named last changes fastest.
The devices are a block of a 8x8x16 slice.
Arguments:
- clip: bfloat16 [128, 32, 64, 512], P(('ga', 'ta'), 'gy'), parts along dimension 0, may hold values from -6 to 6
- w_space: bfloat16 [3, 3, 512, 512], replicated, may hold values from -0.09375 to 0.09375
- w_time: bfloat16 [3, 512, 512], replicated, may hold values from -0.15625 to 0.15625
- w_qkv: bfloat16 [512, 1536], replicated, may hold values from -0.61871843 to 0.61871843
- w_out: bfloat16 [512, 512], replicated, may hold values from -0.25 to 0.25
- norm_gain: float32 [512], replicated, may hold values from 0.1 to 1.9
Outputs:
- block_out: bfloat16 [128, 32, 64, 512], P(('ga', 'ta'), 'gy'), parts along dimension 0
There are 2 independent parts, one for each index of `ga`. A program takes and returns all parts, laid end to end along the dimension named above; an argument that names none is the same for every part. Nothing has to cross between parts.
All inputs are finite; a program needn't handle non-finite values.
Results may differ from a plain program's by a relative error of at most 0.0085.
Values may be sent and summed in bfloat16 or wider, within the bound.
A program may use at most 64 MiB of HBM per device.

v0:
```python
import jax
import jax.numpy as jnp
from jax import lax
from jax.sharding import PartitionSpec as P

HEADS = 8


def padded_2(block, sides, width):
    for axis, dim in sides:
        count = lax.axis_size(axis)
        forward = [(i, i + 1) for i in range(count - 1)]
        backward = [(target, source) for source, target in forward]
        low = lax.ppermute(
            lax.slice_in_dim(block, block.shape[dim] - width, None, axis=dim), axis, forward
        )
        high = lax.ppermute(lax.slice_in_dim(block, 0, width, axis=dim), axis, backward)
        block = jnp.concatenate([low, block, high], axis=dim)
    return block


def from_behind(array, axis, by):
    devices = lax.axis_size(axis)
    pairs = [(i, i + by) for i in range(devices) if 0 <= i + by < devices]
    return lax.ppermute(array, axis, pairs)


def conv_space(padded, w_space, height, width):
    channels = padded.shape[-1]
    total = jnp.zeros(padded.shape[:1] + (height, width, channels), jnp.float32)
    for row_off in range(3):
        for col_off in range(3):
            window = padded[:, row_off : row_off + height, col_off : col_off + width, :]
            product = jnp.dot(
                window.reshape(-1, channels),
                w_space[row_off, col_off],
                preferred_element_type=jnp.float32,
            )
            total = total + product.reshape(total.shape)
    return total


def temporal_mix(clip, hidden, earlier, w_time, norm_gain):
    channels = clip.shape[-1]
    frames = hidden.shape[0]
    joined = jnp.concatenate([earlier, hidden], axis=0)
    total = jnp.zeros(hidden.shape, jnp.float32)
    for tap_index in range(3):
        window = joined[2 - tap_index : 2 - tap_index + frames]
        product = jnp.dot(
            window.reshape(-1, channels), w_time[tap_index], preferred_element_type=jnp.float32
        )
        total = total + product.reshape(hidden.shape)
    mixed = (clip.astype(jnp.float32) + total).astype(jnp.bfloat16)
    wide = mixed.astype(jnp.float32)
    scale = lax.rsqrt(jnp.mean(wide * wide, axis=-1, keepdims=True) + 1e-06)
    normed = (wide * scale * norm_gain).astype(jnp.bfloat16)
    return (mixed, normed)


def project(normed, w_qkv):
    channels = normed.shape[-1]
    flattened = jnp.dot(
        normed.reshape(-1, channels), w_qkv, preferred_element_type=jnp.float32
    ).astype(jnp.bfloat16)
    joined = flattened.reshape(normed.shape[:-1] + (3 * channels,))
    return (
        joined[..., :channels],
        joined[..., channels : 2 * channels],
        joined[..., 2 * channels :],
    )


def attend(queries, keyset, valueset, heads):
    frames, rows, cols, channels = queries.shape
    head_dim = channels // heads
    shape = (frames, rows, cols, heads, head_dim)
    scores = jnp.einsum(
        "frwhd,grwhd->rwhfg",
        queries.reshape(shape),
        keyset.reshape(shape),
        preferred_element_type=jnp.float32,
    )
    scores = scores * (1.0 / head_dim**0.5)
    peak = jnp.max(scores, axis=-1, keepdims=True)
    expo = jnp.exp(scores - peak)
    probs = (expo / jnp.sum(expo, axis=-1, keepdims=True)).astype(jnp.bfloat16)
    output = jnp.einsum(
        "rwhfg,grwhd->frwhd", probs, valueset.reshape(shape), preferred_element_type=jnp.float32
    )
    return output.reshape(queries.shape).astype(jnp.bfloat16)


def attend_back(queries, keyset, valueset):
    output = attend(queries, keyset, valueset, HEADS)
    return lax.all_to_all(output, "ta", split_axis=0, concat_axis=2, tiled=True)


def per_device(clip, w_space, w_time, w_qkv, w_out, norm_gain):
    frames, height, width, channels = clip.shape
    rimmed = padded_2(clip, (("gy", 1),), 1)
    padded = jnp.pad(rimmed, ((0, 0), (0, 0), (1, 1), (0, 0)))
    hidden = jax.nn.silu(conv_space(padded, w_space, height, width)).astype(jnp.bfloat16)
    earlier = from_behind(hidden[-2:], "ta", 1)
    mixed, normed = temporal_mix(clip, hidden, earlier, w_time, norm_gain)
    queries, keyset, valueset = project(
        lax.all_to_all(normed, "ta", split_axis=2, concat_axis=0, tiled=True), w_qkv
    )
    attended = attend_back(queries, keyset, valueset)
    projected = jnp.dot(
        attended.reshape(-1, channels), w_out, preferred_element_type=jnp.float32
    ).reshape(clip.shape)
    return (mixed.astype(jnp.float32) + projected).astype(jnp.bfloat16)


def solution(mesh):
    in_specs = (P(("ga", "ta"), "gy", None, None), P(), P(), P(), P(), P())
    out_specs = P(("ga", "ta"), "gy", None, None)
    return jax.shard_map(
        per_device, mesh=mesh, in_specs=in_specs, out_specs=out_specs, check_vma=False
    )
```

profile of v0, /device:TPU:513, one launch (start us, length us, event | category | flops | bytes accessed | tf_op | source)
XLA Modules:
  0.0 152.4 jit_solution(4100090936141141945)
XLA Ops:
  0.0 1.2 fusion.77
  1.2 4.1 %collective-permute-start = (bf16[4,1,64,512]{3,2,1,0:T(8,128)(2,1)S(1)}, bf16[4,1,64,512]{3,2,1,0:T(8,128)(2,1)S(1)}, u32[]{:S(2)}, u32[]{:S(2)}) collective-permute-start(bf16[4,1,64,512]{3,2,1,0:T(8,128)(2,1)S(1)} %get-tuple-element.8), channel_id=1, source_target_pairs={{0,1},{1,2},{2,3},{3,4},{4,5},{5,6},{6,7},{8,9},{9,10},{10,11},{11... | collective-permute-start | bytes 786440 | tf_op jit(solution)/shard_map/ppermute | solution.py:14
  5.3 1.4 collective-permute-start.1
  6.8 2.2 %fusion.53 = f32[4,4,64,512]{3,2,1,0:T(8,128)S(1)} fusion(bf16[4,4,64,512]{3,2,1,0:T(8,128)(2,1)} %param.6, bf16[3,3,512,512]{3,2,1,0:T(8,128)(2,1)} %param.7), kind=kOutput, calls=%fused_computation.62 | convolution fusion | flops 536870912 | bytes 3670016 | tf_op jit(solution)/shard_map/dot_general | solution.py:34
  9.0 3.6 %collective-permute-done.1 = bf16[4,1,64,512]{3,2,1,0:T(8,128)(2,1)S(1)} collective-permute-done((bf16[4,1,64,512]{3,2,1,0:T(8,128)(2,1)S(1)}, bf16[4,1,64,512]{3,2,1,0:T(8,128)(2,1)S(1)}, u32[]{:S(2)}, u32[]{:S(2)}) %collective-permute-start.1) | collective-permute-done | bytes 262176 | tf_op jit(solution)/shard_map/ppermute | solution.py:17
  18.5 1.4 multiply_convert_fusion
  20.0 7.8 %collective-permute-start.2 = (bf16[2,4,64,512]{3,2,1,0:T(8,128)(2,1)S(1)}, bf16[2,4,64,512]{3,2,1,0:T(8,128)(2,1)S(1)}, u32[]{:S(2)}, u32[]{:S(2)}) collective-permute-start(bf16[2,4,64,512]{3,2,1,0:T(8,128)(2,1)S(1)} %slice.124), channel_id=1, source_target_pairs={{0,8},{8,16},{16,24},{24,32},{32,40},{40,48},{48,56},{56,64},{64,7... | collective-permute-start | bytes 1572872 | tf_op jit(solution)/shard_map/ppermute | solution.py:25
  28.6 12.9 %collective-permute-done.2 = bf16[2,4,64,512]{3,2,1,0:T(8,128)(2,1)S(1)} collective-permute-done((bf16[2,4,64,512]{3,2,1,0:T(8,128)(2,1)S(1)}, bf16[2,4,64,512]{3,2,1,0:T(8,128)(2,1)S(1)}, u32[]{:S(2)}, u32[]{:S(2)}) %collective-permute-start.2) | collective-permute-done | bytes 524320 | tf_op jit(solution)/shard_map/ppermute | solution.py:25
  44.4 34.0 %all_to_all.30 = bf16[4,4,64,512]{3,1,0,2:T(4,128)(2,1)S(1)} all-to-all(bf16[4,4,64,512]{3,1,0,2:T(4,128)(2,1)S(1)} %copy.19), channel_id=1, replica_groups=mesh['ga'=2,'ta'=16,'gy'=8] {'ta'}, dimensions={2} | all-to-all | bytes 2097152 | tf_op jit(solution)/shard_map/all_to_all | solution.py:107
  78.4 1.5 copy.54
  81.0 4.7 %convolution_convert_fusion = bf16[1024,1536]{1,0:T(8,128)(2,1)} fusion(bf16[1024,512]{1,0:T(8,128)(2,1)} %reshape.82, bf16[512,1536]{1,0:T(8,128)(2,1)S(1)} %copy-done), kind=kOutput, calls=%fused_computation.5 | convolution fusion | flops 1612185600 | bytes 5767168 | tf_op jit(solution)/shard_map/dot_general | solution.py:63
  85.6 4.8 %reshape.83 = bf16[64,4,4,1536]{3,2,1,0:T(4,128)(2,1)S(1)} reshape(bf16[1024,1536]{1,0:T(8,128)(2,1)} %convolution_convert_fusion) | data formatting | bytes 6291456 | tf_op jit(solution)/shard_map/reshape | solution.py:66
  90.4 3.0 %fusion.76 = (bf16[64,4,4,512]{3,2,1,0:T(4,128)(2,1)}, bf16[64,4,4,512]{3,2,1,0:T(4,128)(2,1)}, bf16[64,4,4,512]{3,2,1,0:T(4,128)(2,1)}) fusion(bf16[64,4,4,1536]{3,2,1,0:T(4,128)(2,1)S(1)} %reshape.83), kind=kLoop, calls=%fused_computation.86 | loop fusion | bytes 6291456 | tf_op jit(solution)/shard_map/slice | solution.py:68
  93.4 3.1 %reshape.100 = bf16[64,4,4,8,64]{4,3,2,1,0:T(8,128)(2,1)S(1)} reshape(bf16[64,4,4,512]{3,2,1,0:T(4,128)(2,1)} %get-tuple-element.5) | data formatting | bytes 2097152 | tf_op jit(solution)/shard_map/reshape | solution.py:80
  96.5 2.0 %reshape.101 = bf16[64,4,4,8,64]{4,3,2,1,0:T(8,128)(2,1)} reshape(bf16[64,4,4,512]{3,2,1,0:T(4,128)(2,1)S(1)} %copy-done.6) | data formatting | bytes 2097152 | tf_op jit(solution)/shard_map/reshape | solution.py:81
  98.5 4.1 %fusion.10 = f32[4,4,8,64,64]{3,4,2,1,0:T(8,128)S(1)} fusion(bf16[64,4,4,8,64]{4,3,2,1,0:T(8,128)(2,1)} %reshape.101, bf16[64,4,4,8,64]{4,3,2,1,0:T(8,128)(2,1)S(1)} %reshape.100), kind=kOutput, calls=%fused_computation.17 | convolution fusion | flops 67108864 | bytes 4194304 | tf_op jit(solution)/shard_map/frwhd,grwhd->rwhfg/dot_general | solution.py:78
  102.7 3.1 %fusion.78 = (f32[4,4,8,64]{3,2,1,0:T(8,128)S(1)}, f32[4,4,8,64,64]{3,4,2,1,0:T(8,128)}) fusion(f32[4,4,8,64,64]{3,4,2,1,0:T(8,128)S(1)} %fusion.10), kind=kOutput, calls=%fused_computation.88 | output fusion | flops 2097215 | bytes 4227072 | tf_op jit(solution)/shard_map/sub | solution.py:86
  105.8 1.5 copy.21
  107.3 4.2 %fusion.18 = bf16[4,4,8,64,64]{4,3,2,1,0:T(8,128)(2,1)} fusion(bf16[64,4,4,8,64]{0,4,3,2,1:T(8,128)(2,1)S(1)} %bitcast.111, f32[4,4,8,64,64]{3,4,2,1,0:T(8,128)} %get-tuple-element.13, f32[4,4,8,64]{3,2,1,0:T(8,128)S(1)} %get-tuple-element.12), kind=kOutput, calls=%fused_computation.27 | convolution fusion | flops 68681728 | bytes 4227072 | tf_op jit(solution)/shard_map/rwhfg,grwhd->frwhd/dot_general | solution.py:88
  111.5 2.9 %copy.27 = bf16[64,4,4,512]{3,2,1,0:T(4,128)(2,1)S(1)} copy(bf16[64,4,4,512]{0,3,2,1:T(8,128)(2,1)} %bitcast.112) | data formatting | bytes 2097152 | tf_op jit(solution)/shard_map/convert_element_type | solution.py:91
  114.4 31.2 %all_to_all.31 = bf16[64,4,4,512]{3,2,1,0:T(4,128)(2,1)S(1)} all-to-all(bf16[64,4,4,512]{3,2,1,0:T(4,128)(2,1)S(1)} %copy.27), channel_id=1, replica_groups=mesh['ga'=2,'ta'=16,'gy'=8] {'ta'}, dimensions={0} | all-to-all | bytes 2097152 | tf_op jit(solution)/shard_map/all_to_all | solution.py:96
  145.7 1.5 copy.28
  147.2 2.3 %dot_general.65 = bf16[4,4,64,512]{3,2,1,0:T(8,128)(2,1)} reshape(bf16[4,4,16,4,512]{4,3,2,1,0:T(4,128)(2,1)} %copy.28) | data formatting | bytes 2097152 | tf_op jit(solution)/shard_map/dot_general | solution.py:110
  149.5 2.9 %fusion.8 = bf16[4,4,64,512]{3,2,1,0:T(8,128)(2,1)} fusion(bf16[4,4,64,512]{3,2,1,0:T(8,128)(2,1)S(1)} %copy-done.4, bf16[4,4,64,512]{3,2,1,0:T(8,128)(2,1)} %dot_general.65, bf16[512,512]{1,0:T(8,128)(2,1)S(1)} %copy-done.10), kind=kOutput, calls=%fused_computation.15 | convolution fusion | flops 538443776 | bytes 3670016 | tf_op jit(solution)/shard_map/dot_general | solution.py:110
  (39 shorter events, 10.6 us)
Async XLA Ops:
  0.0 81.0 %copy-start = (bf16[512,1536]{1,0:T(8,128)(2,1)S(1)}, bf16[512,1536]{1,0:T(8,128)(2,1)}, u32[]{:S(2)}) copy-start(bf16[512,1536]{1,0:T(8,128)(2,1)} %param.9) | copy-start | bytes 4718596
  1.2 7.8 %collective-permute-start = (bf16[4,1,64,512]{3,2,1,0:T(8,128)(2,1)S(1)}, bf16[4,1,64,512]{3,2,1,0:T(8,128)(2,1)S(1)}, u32[]{:S(2)}, u32[]{:S(2)}) collective-permute-start(bf16[4,1,64,512]{3,2,1,0:T(8,128)(2,1)S(1)} %get-tuple-element.8), channel_id=1, source_target_pairs={{0,1},{1,2},{2,3},{3,4},{4,5},{5,6},{6,7},{8,9},{9,10},{10,11},{11... | collective-permute-start | bytes 786440 | tf_op jit(solution)/shard_map/ppermute | solution.py:14
  5.3 7.3 %copy-start.2 = (bf16[4,4,64,512]{3,2,1,0:T(8,128)(2,1)S(1)}, bf16[4,4,64,512]{3,2,1,0:T(8,128)(2,1)}, u32[]{:S(2)}) copy-start(bf16[4,4,64,512]{3,2,1,0:T(8,128)(2,1)} %param.6) | copy-start | bytes 3145732
  5.3 7.3 %collective-permute-start.1 = (bf16[4,1,64,512]{3,2,1,0:T(8,128)(2,1)S(1)}, bf16[4,1,64,512]{3,2,1,0:T(8,128)(2,1)S(1)}, u32[]{:S(2)}, u32[]{:S(2)}) collective-permute-start(bf16[4,1,64,512]{3,2,1,0:T(8,128)(2,1)S(1)} %get-tuple-element.9), channel_id=1, source_target_pairs={{1,0},{2,1},{3,2},{4,3},{5,4},{6,5},{7,6},{9,8},{10,9},{11,10},{12... | collective-permute-start | bytes 786440 | tf_op jit(solution)/shard_map/ppermute | solution.py:17
  6.8 6.8 %copy-start.7 = (bf16[3,3,512,512]{3,2,1,0:T(8,128)(2,1)S(1)}, bf16[3,3,512,512]{3,2,1,0:T(8,128)(2,1)}, u32[]{:S(2)}) copy-start(bf16[3,3,512,512]{3,2,1,0:T(8,128)(2,1)} %param.7) | copy-start | bytes 14155780
  18.5 9.3 %copy-start.8 = (bf16[3,512,512]{2,1,0:T(8,128)(2,1)S(1)}, bf16[3,512,512]{2,1,0:T(8,128)(2,1)}, u32[]{:S(2)}) copy-start(bf16[3,512,512]{2,1,0:T(8,128)(2,1)} %param.8) | copy-start | bytes 4718596
  20.0 21.5 %collective-permute-start.2 = (bf16[2,4,64,512]{3,2,1,0:T(8,128)(2,1)S(1)}, bf16[2,4,64,512]{3,2,1,0:T(8,128)(2,1)S(1)}, u32[]{:S(2)}, u32[]{:S(2)}) collective-permute-start(bf16[2,4,64,512]{3,2,1,0:T(8,128)(2,1)S(1)} %slice.124), channel_id=1, source_target_pairs={{0,8},{8,16},{16,24},{24,32},{32,40},{40,48},{48,56},{56,64},{64,7... | collective-permute-start | bytes 1572872 | tf_op jit(solution)/shard_map/ppermute | solution.py:25
  42.2 1.0 copy-start.9
  43.2 1.2 copy-start.3
  93.4 3.1 %copy-start.6 = (bf16[64,4,4,512]{3,2,1,0:T(4,128)(2,1)S(1)}, bf16[64,4,4,512]{3,2,1,0:T(4,128)(2,1)}, u32[]{:S(2)}) copy-start(bf16[64,4,4,512]{3,2,1,0:T(4,128)(2,1)} %get-tuple-element.6) | copy-start | bytes 3145732
  102.7 3.1 %copy-start.5 = (bf16[64,4,4,512]{3,2,1,0:T(4,128)(2,1)S(1)}, bf16[64,4,4,512]{3,2,1,0:T(4,128)(2,1)}, u32[]{:S(2)}) copy-start(bf16[64,4,4,512]{3,2,1,0:T(4,128)(2,1)} %get-tuple-element.7) | copy-start | bytes 3145732
  145.7 3.8 %copy-start.4 = (bf16[4,4,64,512]{3,2,1,0:T(8,128)(2,1)S(1)}, bf16[4,4,64,512]{3,2,1,0:T(8,128)(2,1)}, u32[]{:S(2)}) copy-start(bf16[4,4,64,512]{3,2,1,0:T(8,128)(2,1)} %copy-done.3) | copy-start | bytes 3145732
  145.7 3.8 %copy-start.10 = (bf16[512,512]{1,0:T(8,128)(2,1)S(1)}, bf16[512,512]{1,0:T(8,128)(2,1)}, u32[]{:S(2)}) copy-start(bf16[512,512]{1,0:T(8,128)(2,1)} %param.10) | copy-start | bytes 1572868
  147.2 5.2 %copy-start.1 = (bf16[512,1536]{1,0:T(8,128)(2,1)S(1)}, bf16[512,1536]{1,0:T(8,128)(2,1)}, u32[]{:S(2)}) copy-start(bf16[512,1536]{1,0:T(8,128)(2,1)} %param.9) | copy-start | bytes 4718596
where the time goes:
time: 155 us; the launch traced here: 152 us
  blocking collectives  65.2 us (42%)
  matrix products  26.9 us (17%)
  local copies, waits for them, and re-layouts  25.8 us (17%)
  waiting for transfers between devices  16.5 us (11%)
  starting transfers between devices  13.4 us (9%)
  other arithmetic  4.37 us (3%)
    all_to_all x1, blocking collectives, per_device(): lax.all_to_all(normed, 'ta', split_axis=2, concat_axis=0, tiled=True)  34 us
    all_to_all x1, blocking collectives, attend_back(): return lax.all_to_all(output, 'ta', split_axis=0, concat_axis=2, tiled=True)  31.2 us
    ppermute x1, waiting for transfers between devices, from_behind(): return lax.ppermute(array, axis, pairs)  12.9 us
    dot_general x9, matrix products, conv_space(): jnp.dot(window.reshape(-1, channels), w_space[row_off, col_off], preferre...  8.58 us
    ppermute x1, starting transfers between devices, from_behind(): return lax.ppermute(array, axis, pairs)  7.83 us
    reshape x1, local copies, waits for them, and re-layouts, project(): joined = flattened.reshape(normed.shape[:-1] + (3 * channels,))  4.8 us
    dot_general x1, matrix products, project(): jnp.dot(normed.reshape(-1, channels), w_qkv, preferred_element_type=jnp.f...  4.65 us
    dot_general x1, matrix products, attend(): jnp.einsum('rwhfg,grwhd->frwhd', probs, valueset.reshape(shape), preferre...  4.21 us
  transfers between devices with their start and end apart: 3, of which 2 were waited for; matrix products, arithmetic and copies ran while one was open for 2% of the time, Pallas kernels for 0%

commit v1 on v0

v1 whole, which is shorter than its diff:
```python
import functools

import jax
import jax.numpy as jnp
from jax import lax
from jax.experimental import pallas as pl
from jax.experimental.pallas import tpu as pltpu
from jax.sharding import PartitionSpec as P

HEADS = 8
MESH = pl.DeviceIdType.MESH
F32 = jnp.float32
BF16 = jnp.bfloat16


def dot(a, b):
    return jnp.dot(a, b, preferred_element_type=F32)


def dot_t(a, b):
    return lax.dot_general(a, b, (((1,), (1,)), ((), ())), preferred_element_type=F32)


def block_kernel(
    n,
    ny,
    clip,
    w_space,
    w_time,
    w_qkv,
    w_out,
    gain,
    out,
    xv,
    hv,
    mixed,
    sv,
    rv,
    av,
    ov,
    qkv,
    bias,
    perm,
    outv,
    ws,
    wt,
    wq,
    wo,
    gv,
    clip_sem,
    ws_sem,
    w_sem,
    x_send,
    x_recv,
    h_send,
    h_recv,
    a_send,
    a_recv,
    b_send,
    b_recv,
    o_sem,
):
    frames, rows, width, channels = clip.shape
    tokens = frames * width
    cols = width // n
    piece = frames * cols
    t = lax.axis_index("ta")
    g = lax.axis_index("gy")
    chips = n // 2
    chip, core = t // 2, lax.rem(t, 2)

    def peer(chip_off, core_off):
        return lax.rem(chip + chip_off + chips, chips) * 2 + lax.rem(core + core_off, 2)

    half = chips // 2
    offsets = [half]
    for d in range(half - 1, 0, -1):
        offsets += [d, -d]
    peers = [(c, k) for c in offsets for k in (0, 1)] + [(0, 1)]

    barrier = pltpu.get_barrier_semaphore()
    for c, k in peers:
        pl.semaphore_signal(barrier, inc=1, device_id={"ta": peer(c, k)}, device_id_type=MESH)

    @pl.when(g > 0)
    def _():
        pl.semaphore_signal(barrier, inc=1, device_id={"gy": g - 1}, device_id_type=MESH)

    @pl.when(g < ny - 1)
    def _():
        pl.semaphore_signal(barrier, inc=1, device_id={"gy": g + 1}, device_id_type=MESH)

    clip_loads = [
        pltpu.make_async_copy(clip.at[:, r], xv.at[r + 1], clip_sem.at[r]) for r in range(rows)
    ]
    for load in clip_loads:
        load.start()
    space_loads = []
    for b in range(3):
        for a in range(3):
            load = pltpu.make_async_copy(
                w_space.at[a, b], ws.at[b, pl.ds(a * channels, channels)], ws_sem.at[b, a]
            )
            load.start()
            space_loads.append(load)
    other_loads = [
        pltpu.make_async_copy(w_time, wt, w_sem.at[0]),
        pltpu.make_async_copy(w_qkv, wq, w_sem.at[1]),
        pltpu.make_async_copy(w_out, wo, w_sem.at[2]),
        pltpu.make_async_copy(gain, gv, w_sem.at[3]),
    ]
    for load in other_loads:
        load.start()

    row_i = lax.broadcasted_iota(jnp.int32, (tokens, tokens), 0)
    col_i = lax.broadcasted_iota(jnp.int32, (tokens, tokens), 1)
    same = lax.rem(row_i, cols) == lax.rem(col_i, cols)
    bias[...] = jnp.where(same, 0.0, -1e30)
    natural = (
        lax.rem(row_i // cols, frames) * width + (row_i // piece) * cols + lax.rem(row_i, cols)
    )
    perm[0] = jnp.where(natural == col_i, 1.0, 0.0).astype(BF16)
    natural_t = (
        lax.rem(col_i // cols, frames) * width + (col_i // piece) * cols + lax.rem(col_i, cols)
    )
    perm[1] = jnp.where(natural_t == row_i, 1.0, 0.0).astype(BF16)

    @pl.when(g == 0)
    def _():
        xv[0] = jnp.zeros(xv.shape[1:], BF16)

    @pl.when(g == ny - 1)
    def _():
        xv[rows + 1] = jnp.zeros(xv.shape[1:], BF16)

    @pl.when(t == 0)
    def _():
        hv[:, 0:2] = jnp.zeros((rows, 2) + hv.shape[2:], BF16)

    column = lax.rem(lax.broadcasted_iota(jnp.int32, (tokens, channels), 0), width)

    def conv_row(r):
        lhs = jnp.concatenate([xv[r + a].reshape(tokens, channels) for a in range(3)], axis=1)
        left = pltpu.roll(dot(lhs, ws[0]), 1, 0)
        total = jnp.where(column == 0, 0.0, left) + dot(lhs, ws[1])
        right = pltpu.roll(dot(lhs, ws[2]), tokens - 1, 0)
        total = total + jnp.where(column == width - 1, 0.0, right)
        hidden = (total * jax.nn.sigmoid(total)).astype(BF16)
        hv[r, 2:] = hidden.reshape(frames, width, channels)

    def hidden_copy(r):
        return pltpu.make_async_remote_copy(
            src_ref=hv.at[r, pl.ds(frames, 2)],
            dst_ref=hv.at[r, pl.ds(0, 2)],
            send_sem=h_send.at[r],
            recv_sem=h_recv.at[r],
            device_id={"ta": lax.rem(t + 1, n)},
            device_id_type=MESH,
        )

    def send_hidden(r):
        @pl.when(t < n - 1)
        def _():
            hidden_copy(r).start()

    def exchange(src, dst, r, dest, send_sem, recv_sem):
        return pltpu.make_async_remote_copy(
            src_ref=src.at[r, pl.ds(pl.multiple_of(dest * piece, piece), piece)],
            dst_ref=dst.at[r, pl.ds(pl.multiple_of(t * piece, piece), piece)],
            send_sem=send_sem.at[r],
            recv_sem=recv_sem.at[r],
            device_id={"ta": dest},
            device_id_type=MESH,
        )

    def send_all(src, dst, r, send_sem, recv_sem):
        for c, k in peers:
            exchange(src, dst, r, peer(c, k), send_sem, recv_sem).start()
        own = pl.ds(pl.multiple_of(t * piece, piece), piece)
        dst[r, own] = src[r, own]

    def whole(src, dst, r, send_sem, recv_sem):
        return pltpu.make_async_remote_copy(
            src_ref=src.at[r, pl.ds(0, (n - 1) * piece)],
            dst_ref=dst.at[r, pl.ds(0, (n - 1) * piece)],
            send_sem=send_sem.at[r],
            recv_sem=recv_sem.at[r],
            device_id={"ta": lax.rem(t + 1, n)},
            device_id_type=MESH,
        )

    def temporal_row(r):
        @pl.when(t > 0)
        def _():
            hidden_copy(r).wait_recv()

        lhs = jnp.concatenate(
            [hv[r, 2 - k : 2 - k + frames].reshape(tokens, channels) for k in range(3)], axis=1
        )
        total = xv[r + 1].reshape(tokens, channels).astype(F32) + dot(lhs, wt[...])
        rounded = total.astype(BF16)
        mixed[r] = rounded
        wide = rounded.astype(F32)
        scale = lax.rsqrt(jnp.mean(wide * wide, axis=-1, keepdims=True) + 1e-06)
        normed = (wide * scale * gv[...]).astype(BF16)
        sv[r] = dot(perm[0], normed).astype(BF16)
        send_all(sv, rv, r, a_send, a_recv)

    for load in clip_loads + space_loads:
        load.wait()
    lax.fori_loop(1, rows - 1, lambda r, c: (conv_row(r), c)[1], 0)
    for load in other_loads:
        load.wait()

    greeted = n - 1 + jnp.where(g > 0, 1, 0) + jnp.where(g < ny - 1, 1, 0)
    pl.semaphore_wait(barrier, greeted)

    up = pltpu.make_async_remote_copy(
        src_ref=xv.at[1],
        dst_ref=xv.at[rows + 1],
        send_sem=x_send.at[0],
        recv_sem=x_recv.at[0],
        device_id={"gy": lax.rem(g + ny - 1, ny)},
        device_id_type=MESH,
    )
    down = pltpu.make_async_remote_copy(
        src_ref=xv.at[rows],
        dst_ref=xv.at[0],
        send_sem=x_send.at[1],
        recv_sem=x_recv.at[1],
        device_id={"gy": lax.rem(g + 1, ny)},
        device_id_type=MESH,
    )

    @pl.when(g > 0)
    def _():
        up.start()

    @pl.when(g < ny - 1)
    def _():
        down.start()

    for r in range(1, rows - 1):
        send_hidden(r)
    lax.fori_loop(1, rows - 1, lambda r, c: (temporal_row(r), c)[1], 0)

    @pl.when(g > 0)
    def _():
        down.wait_recv()

    @pl.when(g < ny - 1)
    def _():
        up.wait_recv()

    def edge(i, c):
        r = i * (rows - 1)
        conv_row(r)
        send_hidden(r)
        return c

    lax.fori_loop(0, 2, edge, 0)
    lax.fori_loop(0, 2, lambda i, c: (temporal_row(i * (rows - 1)), c)[1], 0)

    lane = lax.broadcasted_iota(jnp.int32, (tokens, 128), 1)
    head_dim = channels // HEADS

    def order(i):
        return jnp.where(i < rows - 2, i + 1, (i - (rows - 2)) * (rows - 1))

    def attend_row(i, carry):
        r = order(i)
        whole(sv, rv, r, a_send, a_recv).wait_recv()
        qkv[...] = dot(rv[r], wq[...]).astype(BF16)

        def pair(p, c):
            base = pl.multiple_of(p * 128, 128)
            q = qkv[:, pl.ds(base, 128)]
            k = qkv[:, pl.ds(pl.multiple_of(channels + p * 128, 128), 128)]
            v = qkv[:, pl.ds(pl.multiple_of(2 * channels + p * 128, 128), 128)]
            results = []
            for h in range(2):
                mine = (lane >= head_dim) if h else (lane < head_dim)
                q_h = jnp.where(mine, q, jnp.zeros_like(q))
                scores = dot_t(q_h, k) * (1.0 / head_dim**0.5) + bias[...]
                peak = jnp.max(scores, axis=-1, keepdims=True)
                expo = jnp.exp(scores - peak)
                total = jnp.sum(expo, axis=-1, keepdims=True)
                probs = (expo * (1.0 / total)).astype(BF16)
                results.append(dot(probs, v))
            av[r, :, pl.ds(base, 128)] = jnp.where(
                lane < head_dim, results[0], results[1]
            ).astype(BF16)
            return c

        lax.fori_loop(0, channels // 128, pair, 0)
        send_all(av, ov, r, b_send, b_recv)
        return carry

    lax.fori_loop(0, rows, attend_row, 0)

    def store(r):
        return pltpu.make_async_copy(outv.at[r], out.at[:, r], o_sem.at[r])

    def out_row(i, carry):
        r = order(i)
        whole(av, ov, r, b_send, b_recv).wait_recv()
        attended = dot(perm[1], ov[r]).astype(BF16)
        total = mixed[r].astype(F32) + dot(attended, wo[...])
        outv[r] = total.astype(BF16).reshape(frames, width, channels)
        store(r).start()
        return carry

    lax.fori_loop(0, rows, out_row, 0)

    @pl.when(g > 0)
    def _():
        up.wait_send()

    @pl.when(g < ny - 1)
    def _():
        down.wait_send()

    for r in range(rows):

        @pl.when(t < n - 1)
        def _():
            hidden_copy(r).wait_send()

        whole(sv, rv, r, a_send, a_recv).wait_send()
        whole(av, ov, r, b_send, b_recv).wait_send()
        store(r).wait()


def solution(mesh):
    n, ny = mesh.shape["ta"], mesh.shape["gy"]

    def per_device(clip, w_space, w_time, w_qkv, w_out, norm_gain):
        frames, rows, width, channels = clip.shape
        tokens = frames * width
        row_tokens = (rows, tokens, channels)
        dma = pltpu.SemaphoreType.DMA
        return pl.pallas_call(
            functools.partial(block_kernel, n, ny),
            out_shape=jax.ShapeDtypeStruct(clip.shape, BF16),
            in_specs=[pl.BlockSpec(memory_space=pl.ANY)] * 6,
            out_specs=pl.BlockSpec(memory_space=pl.ANY),
            scratch_shapes=[
                pltpu.VMEM((rows + 2, frames, width, channels), BF16),
                pltpu.VMEM((rows, frames + 2, width, channels), BF16),
                pltpu.VMEM(row_tokens, BF16),
                pltpu.VMEM(row_tokens, BF16),
                pltpu.VMEM(row_tokens, BF16),
                pltpu.VMEM(row_tokens, BF16),
                pltpu.VMEM(row_tokens, BF16),
                pltpu.VMEM((tokens, 3 * channels), BF16),
                pltpu.VMEM((tokens, tokens), F32),
                pltpu.VMEM((2, tokens, tokens), BF16),
                pltpu.VMEM((rows, frames, width, channels), BF16),
                pltpu.VMEM((3, 3 * channels, channels), BF16),
                pltpu.VMEM((3 * channels, channels), BF16),
                pltpu.VMEM((channels, 3 * channels), BF16),
                pltpu.VMEM((channels, channels), BF16),
                pltpu.VMEM((1, channels), F32),
                dma((rows,)),
                dma((3, 3)),
                dma((4,)),
                dma((2,)),
                dma((2,)),
                dma((rows,)),
                dma((rows,)),
                dma((rows,)),
                dma((rows,)),
                dma((rows,)),
                dma((rows,)),
                dma((rows,)),
            ],
            compiler_params=pltpu.CompilerParams(
                collective_id=0, has_side_effects=True, vmem_limit_bytes=48 * 2**20
            ),
        )(
            clip,
            w_space,
            w_time.reshape(3 * channels, channels),
            w_qkv,
            w_out,
            norm_gain.reshape(1, channels),
        )

    in_specs = (P(("ga", "ta"), "gy", None, None), P(), P(), P(), P(), P())
    out_specs = P(("ga", "ta"), "gy", None, None)
    return jax.shard_map(
        per_device, mesh=mesh, in_specs=in_specs, out_specs=out_specs, check_vma=False
    )
```

time: 155 us -> 83.5 us (0.54); the launches traced: 152 us -> 83.2 us
  Pallas kernels: 0 us -> 76.5 us
  blocking collectives: 65.2 us -> 0 us
  matrix products: 26.9 us -> 0 us
  local copies, waits for them, and re-layouts: 25.8 us -> 6.73 us
  waiting for transfers between devices: 16.5 us -> 0 us
  starting transfers between devices: 13.4 us -> 0 us
  other arithmetic: 4.37 us -> 0 us
    pallas_call x0 -> x1, Pallas kernels: none -> 76.5 us  [per_device(): pl.pallas_call(functools.partial(block_kernel, n, ny), out_shape=jax.Shap...]
    all_to_all x2 -> x0, blocking collectives: 65.2 us -> none  [the longest x1 34 us: per_device(): lax.all_to_all(normed, 'ta', split_axis=2, concat_axis=0, tiled=True)]
    dot_general x16 -> x0, matrix products: 26.9 us -> none  [the longest x9 8.58 us: conv_space(): jnp.dot(window.reshape(-1, channels), w_space[row_off, col_off], preferre...]
    ppermute x3 -> x0, waiting for transfers between devices: 16.5 us -> none  [the longest x1 12.9 us: from_behind(): return lax.ppermute(array, axis, pairs)]
    ppermute x3 -> x0, starting transfers between devices: 13.4 us -> none  [the longest x1 7.83 us: from_behind(): return lax.ppermute(array, axis, pairs)]
    reshape x4 -> x0, local copies, waits for them, and re-layouts: 11 us -> none  [the longest x1 4.8 us: project(): joined = flattened.reshape(normed.shape[:-1] + (3 * channels,))]
    unnamed x22 -> x11, local copies, waits for them, and re-layouts: 0.05 us -> 6.73 us
    slice x4 -> x0, local copies, waits for them, and re-layouts: 5.7 us -> none  [the longest x1 3 us: project(): joined[..., :channels]]
  transfers between devices with their start and end apart: 3 -> 0, of which waited for: 2 -> 0; matrix products, arithmetic and copies ran while one was open for 2% -> 0% of each run, Pallas kernels for 0% -> 0%
where the time goes in v1:
time: 83.5 us; the launch traced here: 83.2 us
  Pallas kernels  76.5 us (92%)
  local copies, waits for them, and re-layouts  6.73 us (8%)
    pallas_call x1, Pallas kernels, per_device(): pl.pallas_call(functools.partial(block_kernel, n, ny), out_shape=jax.Shap...  76.5 us
    unnamed x11, local copies, waits for them, and re-layouts  6.73 us

profile of v1, /device:TPU:513, one launch (start us, length us, event | category | flops | bytes accessed | tf_op | source)
XLA Modules:
  0.0 83.2 jit_solution(15977315871170487673)
XLA Ops:
  0.0 0.0 copy-start
  0.0 1.4 %copy-done = bf16[3,512,512]{2,1,0:T(8,128)(2,1)S(1)} copy-done((bf16[3,512,512]{2,1,0:T(8,128)(2,1)S(1)}, bf16[3,512,512]{2,1,0:T(8,128)(2,1)}, u32[]{:S(2)}) %copy-start) | copy-done | bytes 1572888
  1.4 0.0 copy-start.1
  1.4 1.4 %copy-done.1 = bf16[512,1536]{1,0:T(8,128)(2,1)S(1)} copy-done((bf16[512,1536]{1,0:T(8,128)(2,1)S(1)}, bf16[512,1536]{1,0:T(8,128)(2,1)}, u32[]{:S(2)}) %copy-start.1) | copy-done | bytes 1572888
  2.8 0.0 copy-start.2
  2.8 1.2 %copy-done.2 = bf16[4,4,64,512]{3,2,1,0:T(8,128)(2,1)S(1)} copy-done((bf16[4,4,64,512]{3,2,1,0:T(8,128)(2,1)S(1)}, bf16[4,4,64,512]{3,2,1,0:T(8,128)(2,1)}, u32[]{:S(2)}) %copy-start.2) | copy-done | bytes 1048600
  4.0 0.0 copy-start.3
  4.0 1.0 %copy-done.3 = bf16[512,512]{1,0:T(8,128)(2,1)S(1)} copy-done((bf16[512,512]{1,0:T(8,128)(2,1)S(1)}, bf16[512,512]{1,0:T(8,128)(2,1)}, u32[]{:S(2)}) %copy-start.3) | copy-done | bytes 524312
  5.1 0.0 copy-start.4
  5.1 0.7 copy-done.4
  5.8 76.5 %shard_map.64 = bf16[4,4,64,512]{3,2,1,0:T(8,128)(2,1)S(1)} custom-call(bf16[4,4,64,512]{3,2,1,0:T(8,128)(2,1)S(1)} %copy-done.2, bf16[3,3,512,512]{3,2,1,0:T(8,128)(2,1)} %w_space.1, bf16[1536,512]{1,0:T(8,128)(2,1)S(1)} %bitcast.2, bf16[512,1536]{1,0:T(8,128)(2,1)S(1)} %copy-done.1, bf16[512,512]{1,0:T(8,128)(2,1)S(1)} %copy-done.3, f32[1,512]{1,0:T(1,128)S(1)} %bitcast.3), custom_call_target="tpu_custom_call" | custom-call | tf_op jit(solution)/shard_map/pallas_call | solution.py:342
  82.3 1.0 %copy.8 = bf16[4,4,64,512]{3,2,1,0:T(8,128)(2,1)} copy(bf16[4,4,64,512]{3,2,1,0:T(8,128)(2,1)S(1)} %shard_map.64) | data formatting | bytes 2097152
Async XLA Ops:
  0.0 1.4 %copy-start = (bf16[3,512,512]{2,1,0:T(8,128)(2,1)S(1)}, bf16[3,512,512]{2,1,0:T(8,128)(2,1)}, u32[]{:S(2)}) copy-start(bf16[3,512,512]{2,1,0:T(8,128)(2,1)} %param.8) | copy-start | bytes 4718596
  1.4 1.4 %copy-start.1 = (bf16[512,1536]{1,0:T(8,128)(2,1)S(1)}, bf16[512,1536]{1,0:T(8,128)(2,1)}, u32[]{:S(2)}) copy-start(bf16[512,1536]{1,0:T(8,128)(2,1)} %w_qkv.1) | copy-start | bytes 4718596
  2.8 1.2 %copy-start.2 = (bf16[4,4,64,512]{3,2,1,0:T(8,128)(2,1)S(1)}, bf16[4,4,64,512]{3,2,1,0:T(8,128)(2,1)}, u32[]{:S(2)}) copy-start(bf16[4,4,64,512]{3,2,1,0:T(8,128)(2,1)} %clip.1) | copy-start | bytes 3145732
  4.0 1.0 %copy-start.3 = (bf16[512,512]{1,0:T(8,128)(2,1)S(1)}, bf16[512,512]{1,0:T(8,128)(2,1)}, u32[]{:S(2)}) copy-start(bf16[512,512]{1,0:T(8,128)(2,1)} %w_out.1) | copy-start | bytes 1572868
  5.1 0.7 copy-start.4

commit v2 on v1

--- a/solution.py
+++ b/solution.py
@@ -41,7 +41,6 @@
     qkv,
     bias,
     perm,
-    outv,
     ws,
     wt,
     wq,
@@ -58,7 +57,8 @@
     a_recv,
     b_send,
     b_recv,
-    o_sem,
+    late,
+    x_ready,
 ):
     frames, rows, width, channels = clip.shape
     tokens = frames * width
@@ -79,16 +79,17 @@
     peers = [(c, k) for c in offsets for k in (0, 1)] + [(0, 1)]
 
     barrier = pltpu.get_barrier_semaphore()
-    for c, k in peers:
-        pl.semaphore_signal(barrier, inc=1, device_id={"ta": peer(c, k)}, device_id_type=MESH)
 
     @pl.when(g > 0)
     def _():
         pl.semaphore_signal(barrier, inc=1, device_id={"gy": g - 1}, device_id_type=MESH)
 
-    @pl.when(g < ny - 1)
-    def _():
-        pl.semaphore_signal(barrier, inc=1, device_id={"gy": g + 1}, device_id_type=MESH)
+    @pl.when(t > 0)
+    def _():
+        for c, k in peers:
+            pl.semaphore_signal(barrier, inc=1, device_id={"ta": peer(c, k)}, device_id_type=MESH)
+
+    above = jnp.where(g < ny - 1, 1, 0)
 
     clip_loads = [
         pltpu.make_async_copy(clip.at[:, r], xv.at[r + 1], clip_sem.at[r]) for r in range(rows)
@@ -112,6 +113,12 @@
     for load in other_loads:
         load.start()
 
+    @pl.when(t == 0)
+    def _():
+        pl.semaphore_wait(barrier, n - 1 + above)
+        for k in range(1, n):
+            pl.semaphore_signal(late, inc=1, device_id={"ta": k}, device_id_type=MESH)
+
     row_i = lax.broadcasted_iota(jnp.int32, (tokens, tokens), 0)
     col_i = lax.broadcasted_iota(jnp.int32, (tokens, tokens), 1)
     same = lax.rem(row_i, cols) == lax.rem(col_i, cols)
@@ -173,9 +180,17 @@
             device_id_type=MESH,
         )
 
-    def send_all(src, dst, r, send_sem, recv_sem):
+    def send_all(src, dst, r, send_sem, recv_sem, skip_first):
         for c, k in peers:
-            exchange(src, dst, r, peer(c, k), send_sem, recv_sem).start()
+            dest = peer(c, k)
+            if skip_first:
+
+                @pl.when(dest > 0)
+                def _():
+                    exchange(src, dst, r, dest, send_sem, recv_sem).start()
+
+            else:
+                exchange(src, dst, r, dest, send_sem, recv_sem).start()
         own = pl.ds(pl.multiple_of(t * piece, piece), piece)
         dst[r, own] = src[r, own]
 
@@ -204,7 +219,7 @@
         scale = lax.rsqrt(jnp.mean(wide * wide, axis=-1, keepdims=True) + 1e-06)
         normed = (wide * scale * gv[...]).astype(BF16)
         sv[r] = dot(perm[0], normed).astype(BF16)
-        send_all(sv, rv, r, a_send, a_recv)
+        send_all(sv, rv, r, a_send, a_recv, True)
 
     for load in clip_loads + space_loads:
         load.wait()
@@ -212,8 +227,9 @@
     for load in other_loads:
         load.wait()
 
-    greeted = n - 1 + jnp.where(g > 0, 1, 0) + jnp.where(g < ny - 1, 1, 0)
-    pl.semaphore_wait(barrier, greeted)
+    @pl.when(t > 0)
+    def _():
+        pl.semaphore_wait(barrier, n - 2 + above)
 
     up = pltpu.make_async_remote_copy(
         src_ref=xv.at[1],
@@ -232,17 +248,20 @@
         device_id_type=MESH,
     )
 
-    @pl.when(g > 0)
-    def _():
-        up.start()
-
-    @pl.when(g < ny - 1)
-    def _():
-        down.start()
-
     for r in range(1, rows - 1):
         send_hidden(r)
-    lax.fori_loop(1, rows - 1, lambda r, c: (temporal_row(r), c)[1], 0)
+
+    @pl.when(g < ny - 1)
+    def _():
+        pl.semaphore_signal(x_ready, inc=1, device_id={"gy": g + 1}, device_id_type=MESH)
+        down.start()
+
+    @pl.when(g > 0)
+    def _():
+        pl.semaphore_wait(x_ready, 1)
+        up.start()
+
+    temporal_row(1)
 
     @pl.when(g > 0)
     def _():
@@ -259,13 +278,20 @@
         return c
 
     lax.fori_loop(0, 2, edge, 0)
-    lax.fori_loop(0, 2, lambda i, c: (temporal_row(i * (rows - 1)), c)[1], 0)
+
+    def order(i):
+        return jnp.where(i < rows - 2, i + 1, (i - (rows - 2)) * (rows - 1))
+
+    lax.fori_loop(1, rows, lambda i, c: (temporal_row(order(i)), c)[1], 0)
+
+    @pl.when(t > 0)
+    def _():
+        pl.semaphore_wait(late, 1)
+        for r in list(range(1, rows - 1)) + [0, rows - 1]:
+            exchange(sv, rv, r, 0, a_send, a_recv).start()
 
     lane = lax.broadcasted_iota(jnp.int32, (tokens, 128), 1)
     head_dim = channels // HEADS
-
-    def order(i):
-        return jnp.where(i < rows - 2, i + 1, (i - (rows - 2)) * (rows - 1))
 
     def attend_row(i, carry):
         r = order(i)
@@ -293,21 +319,17 @@
             return c
 
         lax.fori_loop(0, channels // 128, pair, 0)
-        send_all(av, ov, r, b_send, b_recv)
+        send_all(av, ov, r, b_send, b_recv, False)
         return carry
 
     lax.fori_loop(0, rows, attend_row, 0)
-
-    def store(r):
-        return pltpu.make_async_copy(outv.at[r], out.at[:, r], o_sem.at[r])
 
     def out_row(i, carry):
         r = order(i)
         whole(av, ov, r, b_send, b_recv).wait_recv()
         attended = dot(perm[1], ov[r]).astype(BF16)
         total = mixed[r].astype(F32) + dot(attended, wo[...])
-        outv[r] = total.astype(BF16).reshape(frames, width, channels)
-        store(r).start()
+        out[:, r] = total.astype(BF16).reshape(frames, width, channels)
         return carry
 
     lax.fori_loop(0, rows, out_row, 0)
@@ -328,7 +350,6 @@
 
         whole(sv, rv, r, a_send, a_recv).wait_send()
         whole(av, ov, r, b_send, b_recv).wait_send()
-        store(r).wait()
 
 
 def solution(mesh):
@@ -341,9 +362,9 @@
         dma = pltpu.SemaphoreType.DMA
         return pl.pallas_call(
             functools.partial(block_kernel, n, ny),
-            out_shape=jax.ShapeDtypeStruct(clip.shape, BF16),
-            in_specs=[pl.BlockSpec(memory_space=pl.ANY)] * 6,
-            out_specs=pl.BlockSpec(memory_space=pl.ANY),
+            out_shape=pltpu.VMEM(clip.shape, BF16),
+            in_specs=[pl.BlockSpec(memory_space=pltpu.HBM)] * 6,
+            out_specs=pl.BlockSpec(memory_space=pltpu.VMEM),
             scratch_shapes=[
                 pltpu.VMEM((rows + 2, frames, width, channels), BF16),
                 pltpu.VMEM((rows, frames + 2, width, channels), BF16),
@@ -355,7 +376,6 @@
                 pltpu.VMEM((tokens, 3 * channels), BF16),
                 pltpu.VMEM((tokens, tokens), F32),
                 pltpu.VMEM((2, tokens, tokens), BF16),
-                pltpu.VMEM((rows, frames, width, channels), BF16),
                 pltpu.VMEM((3, 3 * channels, channels), BF16),
                 pltpu.VMEM((3 * channels, channels), BF16),
                 pltpu.VMEM((channels, 3 * channels), BF16),
@@ -372,18 +392,24 @@
                 dma((rows,)),
                 dma((rows,)),
                 dma((rows,)),
-                dma((rows,)),
+                pltpu.SemaphoreType.REGULAR,
+                pltpu.SemaphoreType.REGULAR,
             ],
             compiler_params=pltpu.CompilerParams(
                 collective_id=0, has_side_effects=True, vmem_limit_bytes=48 * 2**20
             ),
         )(
-            clip,
-            w_space,
-            w_time.reshape(3 * channels, channels),
-            w_qkv,
-            w_out,
-            norm_gain.reshape(1, channels),
+            *(
+                pltpu.with_memory_space_constraint(a, pltpu.HBM)
+                for a in (
+                    clip,
+                    w_space,
+                    w_time.reshape(3 * channels, channels),
+                    w_qkv,
+                    w_out,
+                    norm_gain.reshape(1, channels),
+                )
+            )
         )
 
     in_specs = (P(("ga", "ta"), "gy", None, None), P(), P(), P(), P(), P())

time: 83.5 us -> 74.5 us (0.89)
  local copies, waits for them, and re-layouts: 6.73 us -> 0.97 us
  Pallas kernels: 76.5 us -> 73.5 us
    unnamed x11 -> x1, local copies, waits for them, and re-layouts: 6.73 us -> 0.97 us
    pallas_call x1, Pallas kernels: 76.5 us -> 73.5 us  [per_device(): pl.pallas_call(functools.partial(block_kernel, n, ny), out_shape=pltpu.VM...]
where the time goes in v2:
time: 74.5 us; the launch traced here: 74.4 us
  Pallas kernels  73.5 us (99%)
  local copies, waits for them, and re-layouts  0.97 us (1%)
    pallas_call x1, Pallas kernels, per_device(): pl.pallas_call(functools.partial(block_kernel, n, ny), out_shape=pltpu.VM...  73.5 us

profile of v2, /device:TPU:513, one launch (start us, length us, event | category | flops | bytes accessed | tf_op | source)
XLA Modules:
  0.0 74.4 jit_solution(8073817751640667999)
XLA Ops:
  0.0 73.5 %shard_map.64 = bf16[4,4,64,512]{3,2,1,0:T(8,128)(2,1)S(1)} custom-call(bf16[4,4,64,512]{3,2,1,0:T(8,128)(2,1)} %clip.1, bf16[3,3,512,512]{3,2,1,0:T(8,128)(2,1)} %w_space.1, bf16[1536,512]{1,0:T(8,128)(2,1)} %bitcast.2, bf16[512,1536]{1,0:T(8,128)(2,1)} %w_qkv.1, bf16[512,512]{1,0:T(8,128)(2,1)} %w_out.1, f32[1,512]{1,0:T(1,128)} %bitcast.3), custom_call_target="tpu_custom_call" | custom-call | tf_op jit(solution)/shard_map/pallas_call | solution.py:363
  73.5 1.0 %copy.8 = bf16[4,4,64,512]{3,2,1,0:T(8,128)(2,1)} copy(bf16[4,4,64,512]{3,2,1,0:T(8,128)(2,1)S(1)} %shard_map.64) | data formatting | bytes 2097152

commit v3 on v2

--- a/solution.py
+++ b/solution.py
@@ -39,7 +39,11 @@
     av,
     ov,
     qkv,
-    bias,
+    scores,
+    expo,
+    summed,
+    ones,
+    att,
     perm,
     ws,
     wt,
@@ -58,7 +62,8 @@
     b_send,
     b_recv,
     late,
-    x_ready,
+    ready,
+    next_ready,
 ):
     frames, rows, width, channels = clip.shape
     tokens = frames * width
@@ -84,12 +89,19 @@
     def _():
         pl.semaphore_signal(barrier, inc=1, device_id={"gy": g - 1}, device_id_type=MESH)
 
+    @pl.when(g < ny - 1)
+    def _():
+        pl.semaphore_signal(barrier, inc=1, device_id={"gy": g + 1}, device_id_type=MESH)
+
     @pl.when(t > 0)
     def _():
-        for c, k in peers:
-            pl.semaphore_signal(barrier, inc=1, device_id={"ta": peer(c, k)}, device_id_type=MESH)
-
-    above = jnp.where(g < ny - 1, 1, 0)
+        for k in range(n):
+
+            @pl.when((k > t) | (k == 0))
+            def _():
+                pl.semaphore_signal(barrier, inc=1, device_id={"ta": k}, device_id_type=MESH)
+
+    beside = jnp.where(g < ny - 1, 1, 0) + jnp.where(g > 0, 1, 0)
 
     clip_loads = [
         pltpu.make_async_copy(clip.at[:, r], xv.at[r + 1], clip_sem.at[r]) for r in range(rows)
@@ -110,19 +122,10 @@
         pltpu.make_async_copy(w_out, wo, w_sem.at[2]),
         pltpu.make_async_copy(gain, gv, w_sem.at[3]),
     ]
-    for load in other_loads:
-        load.start()
-
-    @pl.when(t == 0)
-    def _():
-        pl.semaphore_wait(barrier, n - 1 + above)
-        for k in range(1, n):
-            pl.semaphore_signal(late, inc=1, device_id={"ta": k}, device_id_type=MESH)
 
     row_i = lax.broadcasted_iota(jnp.int32, (tokens, tokens), 0)
     col_i = lax.broadcasted_iota(jnp.int32, (tokens, tokens), 1)
-    same = lax.rem(row_i, cols) == lax.rem(col_i, cols)
-    bias[...] = jnp.where(same, 0.0, -1e30)
+    clip_len = n * frames
     natural = (
         lax.rem(row_i // cols, frames) * width + (row_i // piece) * cols + lax.rem(row_i, cols)
     )
@@ -131,6 +134,10 @@
         lax.rem(col_i // cols, frames) * width + (col_i // piece) * cols + lax.rem(col_i, cols)
     )
     perm[1] = jnp.where(natural_t == row_i, 1.0, 0.0).astype(BF16)
+    by_col = lax.rem(row_i, clip_len) * cols + row_i // clip_len
+    perm[2] = jnp.where(by_col == col_i, 1.0, 0.0).astype(BF16)
+    by_col_t = lax.rem(col_i, clip_len) * cols + col_i // clip_len
+    perm[3] = jnp.where(by_col_t == row_i, 1.0, 0.0).astype(BF16)
 
     @pl.when(g == 0)
     def _():
@@ -219,20 +226,9 @@
         scale = lax.rsqrt(jnp.mean(wide * wide, axis=-1, keepdims=True) + 1e-06)
         normed = (wide * scale * gv[...]).astype(BF16)
         sv[r] = dot(perm[0], normed).astype(BF16)
-        send_all(sv, rv, r, a_send, a_recv, True)
-
-    for load in clip_loads + space_loads:
-        load.wait()
-    lax.fori_loop(1, rows - 1, lambda r, c: (conv_row(r), c)[1], 0)
-    for load in other_loads:
-        load.wait()
-
-    @pl.when(t > 0)
-    def _():
-        pl.semaphore_wait(barrier, n - 2 + above)
 
     up = pltpu.make_async_remote_copy(
-        src_ref=xv.at[1],
+        src_ref=clip.at[:, 0],
         dst_ref=xv.at[rows + 1],
         send_sem=x_send.at[0],
         recv_sem=x_recv.at[0],
@@ -240,28 +236,69 @@
         device_id_type=MESH,
     )
     down = pltpu.make_async_remote_copy(
-        src_ref=xv.at[rows],
+        src_ref=clip.at[:, rows - 1],
         dst_ref=xv.at[0],
         send_sem=x_send.at[1],
         recv_sem=x_recv.at[1],
         device_id={"gy": lax.rem(g + 1, ny)},
         device_id_type=MESH,
     )
+    pl.semaphore_wait(barrier, jnp.where(t == 0, n - 1, t - 1) + beside)
+
+    @pl.when(g < ny - 1)
+    def _():
+        down.start()
+
+    @pl.when(g > 0)
+    def _():
+        up.start()
+
+    @pl.when(t > 1)
+    def _():
+        pl.semaphore_signal(next_ready, inc=1, device_id={"ta": t - 1}, device_id_type=MESH)
+
+    for k in range(1, n):
+
+        @pl.when(k < t)
+        def _():
+            pl.semaphore_signal(ready, inc=1, device_id={"ta": k}, device_id_type=MESH)
+
+        @pl.when(t == 0)
+        def _():
+            pl.semaphore_signal(late, inc=1, device_id={"ta": k}, device_id_type=MESH)
+
+    for load in clip_loads + space_loads:
+        load.wait()
+    for load in other_loads:
+        load.start()
+    lax.fori_loop(1, rows - 1, lambda r, c: (conv_row(r), c)[1], 0)
+
+    @pl.when((t > 0) & (t < n - 1))
+    def _():
+        pl.semaphore_wait(next_ready, 1)
 
     for r in range(1, rows - 1):
         send_hidden(r)
 
-    @pl.when(g < ny - 1)
-    def _():
-        pl.semaphore_signal(x_ready, inc=1, device_id={"gy": g + 1}, device_id_type=MESH)
-        down.start()
-
-    @pl.when(g > 0)
-    def _():
-        pl.semaphore_wait(x_ready, 1)
-        up.start()
-
-    temporal_row(1)
+    for load in other_loads:
+        load.wait()
+
+    def order(i):
+        return jnp.where(i < rows - 2, i + 1, (i - (rows - 2)) * (rows - 1))
+
+    def temporal(i, c):
+        r = order(i)
+        temporal_row(r)
+
+        @pl.when((i == 0) & (t > 0) & (t < n - 1))
+        def _():
+            pl.semaphore_wait(ready, n - 1 - t)
+
+        send_all(sv, rv, r, a_send, a_recv, True)
+        return c
+
+    before = jnp.where((t == 0) | (t >= n // 2), 1, 0)
+    lax.fori_loop(0, before, temporal, 0)
 
     @pl.when(g > 0)
     def _():
@@ -278,11 +315,7 @@
         return c
 
     lax.fori_loop(0, 2, edge, 0)
-
-    def order(i):
-        return jnp.where(i < rows - 2, i + 1, (i - (rows - 2)) * (rows - 1))
-
-    lax.fori_loop(1, rows, lambda i, c: (temporal_row(order(i)), c)[1], 0)
+    lax.fori_loop(before, rows, temporal, 0)
 
     @pl.when(t > 0)
     def _():
@@ -290,35 +323,45 @@
         for r in list(range(1, rows - 1)) + [0, rows - 1]:
             exchange(sv, rv, r, 0, a_send, a_recv).start()
 
-    lane = lax.broadcasted_iota(jnp.int32, (tokens, 128), 1)
     head_dim = channels // HEADS
+    quad = 4 * head_dim
+    low = lax.broadcasted_iota(jnp.int32, (clip_len, 2 * head_dim), 1) < head_dim
+    head_of = lax.broadcasted_iota(jnp.int32, (clip_len, quad), 1) // head_dim
+    ones_row = lax.broadcasted_iota(jnp.int32, (4 * clip_len, quad), 0) // clip_len
+    ones_col = lax.broadcasted_iota(jnp.int32, (4 * clip_len, quad), 1) // head_dim
+    ones[...] = jnp.where(ones_row == ones_col, 1.0, 0.0).astype(BF16)
+    log2e_scale = 1.4426950408889634 / head_dim**0.5
+    columns = [slice(c * clip_len, (c + 1) * clip_len) for c in range(cols)]
+    quads = [slice(base, base + quad) for base in range(0, channels, quad)]
+
+    def split_heads(x):
+        zero = jnp.zeros_like(x)
+        return jnp.concatenate([jnp.where(head_of == h, x, zero) for h in range(4)], axis=0)
 
     def attend_row(i, carry):
         r = order(i)
         whole(sv, rv, r, a_send, a_recv).wait_recv()
-        qkv[...] = dot(rv[r], wq[...]).astype(BF16)
-
-        def pair(p, c):
-            base = pl.multiple_of(p * 128, 128)
-            q = qkv[:, pl.ds(base, 128)]
-            k = qkv[:, pl.ds(pl.multiple_of(channels + p * 128, 128), 128)]
-            v = qkv[:, pl.ds(pl.multiple_of(2 * channels + p * 128, 128), 128)]
-            results = []
-            for h in range(2):
-                mine = (lane >= head_dim) if h else (lane < head_dim)
-                q_h = jnp.where(mine, q, jnp.zeros_like(q))
-                scores = dot_t(q_h, k) * (1.0 / head_dim**0.5) + bias[...]
-                peak = jnp.max(scores, axis=-1, keepdims=True)
-                expo = jnp.exp(scores - peak)
-                total = jnp.sum(expo, axis=-1, keepdims=True)
-                probs = (expo * (1.0 / total)).astype(BF16)
-                results.append(dot(probs, v))
-            av[r, :, pl.ds(base, 128)] = jnp.where(
-                lane < head_dim, results[0], results[1]
-            ).astype(BF16)
-            return c
-
-        lax.fori_loop(0, channels // 128, pair, 0)
+        arrived = dot(perm[2], rv[r]).astype(BF16)
+        qkv[...] = dot(arrived, wq[...]).astype(BF16)
+        for here in columns:
+            for four in quads:
+                k = qkv[here, channels + four.start : channels + four.stop]
+                scores[here, four] = dot_t(qkv[here, four], split_heads(k))
+        for here in columns:
+            for base in range(0, channels, 2 * head_dim):
+                pair = slice(base, base + 2 * head_dim)
+                s = scores[here, pair]
+                peak_low = jnp.max(jnp.where(low, s, -jnp.inf), axis=-1, keepdims=True)
+                peak_high = jnp.max(jnp.where(low, -jnp.inf, s), axis=-1, keepdims=True)
+                peak = jnp.where(low, peak_low, peak_high)
+                expo[here, pair] = jnp.exp2((s - peak) * log2e_scale).astype(BF16)
+        for four in quads:
+            for here in columns:
+                v = qkv[here, 2 * channels + four.start : 2 * channels + four.stop]
+                summed[here, four] = dot(expo[here, four], split_heads(v))
+            total = dot(expo[:, four], ones[...])
+            att[:, four] = (summed[:, four] / total).astype(BF16)
+        av[r] = dot(perm[3], att[...]).astype(BF16)
         send_all(av, ov, r, b_send, b_recv, False)
         return carry
 
@@ -374,8 +417,12 @@
                 pltpu.VMEM(row_tokens, BF16),
                 pltpu.VMEM(row_tokens, BF16),
                 pltpu.VMEM((tokens, 3 * channels), BF16),
-                pltpu.VMEM((tokens, tokens), F32),
-                pltpu.VMEM((2, tokens, tokens), BF16),
+                pltpu.VMEM((tokens, channels), F32),
+                pltpu.VMEM((tokens, channels), BF16),
+                pltpu.VMEM((tokens, channels), F32),
+                pltpu.VMEM((4 * n * frames, 4 * (channels // HEADS)), BF16),
+                pltpu.VMEM((tokens, channels), BF16),
+                pltpu.VMEM((4, tokens, tokens), BF16),
                 pltpu.VMEM((3, 3 * channels, channels), BF16),
                 pltpu.VMEM((3 * channels, channels), BF16),
                 pltpu.VMEM((channels, 3 * channels), BF16),
@@ -392,6 +439,7 @@
                 dma((rows,)),
                 dma((rows,)),
                 dma((rows,)),
+                pltpu.SemaphoreType.REGULAR,
                 pltpu.SemaphoreType.REGULAR,
                 pltpu.SemaphoreType.REGULAR,
             ],

time: 74.5 us -> 70.5 us (0.946)
  Pallas kernels: 73.5 us -> 69.4 us
    pallas_call x1, Pallas kernels: 73.5 us -> 69.4 us  [per_device(): pl.pallas_call(functools.partial(block_kernel, n, ny), out_shape=pltpu.VM...]
where the time goes in v3:
time: 70.5 us; the launch traced here: 70.4 us
  Pallas kernels  69.4 us (98%)
  local copies, waits for them, and re-layouts  0.97 us (1%)
    pallas_call x1, Pallas kernels, per_device(): pl.pallas_call(functools.partial(block_kernel, n, ny), out_shape=pltpu.VM...  69.4 us

profile of v3, /device:TPU:513, one launch (start us, length us, event | category | flops | bytes accessed | tf_op | source)
XLA Modules:
  0.0 70.4 jit_solution(13784456397012946231)
XLA Ops:
  0.0 69.4 %shard_map.64 = bf16[4,4,64,512]{3,2,1,0:T(8,128)(2,1)S(1)} custom-call(bf16[4,4,64,512]{3,2,1,0:T(8,128)(2,1)} %clip.1, bf16[3,3,512,512]{3,2,1,0:T(8,128)(2,1)} %w_space.1, bf16[1536,512]{1,0:T(8,128)(2,1)} %bitcast.2, bf16[512,1536]{1,0:T(8,128)(2,1)} %w_qkv.1, bf16[512,512]{1,0:T(8,128)(2,1)} %w_out.1, f32[1,512]{1,0:T(1,128)} %bitcast.3), custom_call_target="tpu_custom_call" | custom-call | tf_op jit(solution)/shard_map/pallas_call | solution.py:406
  69.4 1.0 %copy.8 = bf16[4,4,64,512]{3,2,1,0:T(8,128)(2,1)} copy(bf16[4,4,64,512]{3,2,1,0:T(8,128)(2,1)S(1)} %shard_map.64) | data formatting | bytes 2097152

commit v4 on v3

--- a/solution.py
+++ b/solution.py
@@ -64,6 +64,9 @@
     late,
     ready,
     next_ready,
+    passing,
+    pass_send,
+    pass_recv,
 ):
     frames, rows, width, channels = clip.shape
     tokens = frames * width
@@ -78,6 +81,7 @@
         return lax.rem(chip + chip_off + chips, chips) * 2 + lax.rem(core + core_off, 2)
 
     half = chips // 2
+    early = 2 * (chips - 1 - half)
     offsets = [half]
     for d in range(half - 1, 0, -1):
         offsets += [d, -d]
@@ -123,110 +127,6 @@
         pltpu.make_async_copy(gain, gv, w_sem.at[3]),
     ]
 
-    row_i = lax.broadcasted_iota(jnp.int32, (tokens, tokens), 0)
-    col_i = lax.broadcasted_iota(jnp.int32, (tokens, tokens), 1)
-    clip_len = n * frames
-    natural = (
-        lax.rem(row_i // cols, frames) * width + (row_i // piece) * cols + lax.rem(row_i, cols)
-    )
-    perm[0] = jnp.where(natural == col_i, 1.0, 0.0).astype(BF16)
-    natural_t = (
-        lax.rem(col_i // cols, frames) * width + (col_i // piece) * cols + lax.rem(col_i, cols)
-    )
-    perm[1] = jnp.where(natural_t == row_i, 1.0, 0.0).astype(BF16)
-    by_col = lax.rem(row_i, clip_len) * cols + row_i // clip_len
-    perm[2] = jnp.where(by_col == col_i, 1.0, 0.0).astype(BF16)
-    by_col_t = lax.rem(col_i, clip_len) * cols + col_i // clip_len
-    perm[3] = jnp.where(by_col_t == row_i, 1.0, 0.0).astype(BF16)
-
-    @pl.when(g == 0)
-    def _():
-        xv[0] = jnp.zeros(xv.shape[1:], BF16)
-
-    @pl.when(g == ny - 1)
-    def _():
-        xv[rows + 1] = jnp.zeros(xv.shape[1:], BF16)
-
-    @pl.when(t == 0)
-    def _():
-        hv[:, 0:2] = jnp.zeros((rows, 2) + hv.shape[2:], BF16)
-
-    column = lax.rem(lax.broadcasted_iota(jnp.int32, (tokens, channels), 0), width)
-
-    def conv_row(r):
-        lhs = jnp.concatenate([xv[r + a].reshape(tokens, channels) for a in range(3)], axis=1)
-        left = pltpu.roll(dot(lhs, ws[0]), 1, 0)
-        total = jnp.where(column == 0, 0.0, left) + dot(lhs, ws[1])
-        right = pltpu.roll(dot(lhs, ws[2]), tokens - 1, 0)
-        total = total + jnp.where(column == width - 1, 0.0, right)
-        hidden = (total * jax.nn.sigmoid(total)).astype(BF16)
-        hv[r, 2:] = hidden.reshape(frames, width, channels)
-
-    def hidden_copy(r):
-        return pltpu.make_async_remote_copy(
-            src_ref=hv.at[r, pl.ds(frames, 2)],
-            dst_ref=hv.at[r, pl.ds(0, 2)],
-            send_sem=h_send.at[r],
-            recv_sem=h_recv.at[r],
-            device_id={"ta": lax.rem(t + 1, n)},
-            device_id_type=MESH,
-        )
-
-    def send_hidden(r):
-        @pl.when(t < n - 1)
-        def _():
-            hidden_copy(r).start()
-
-    def exchange(src, dst, r, dest, send_sem, recv_sem):
-        return pltpu.make_async_remote_copy(
-            src_ref=src.at[r, pl.ds(pl.multiple_of(dest * piece, piece), piece)],
-            dst_ref=dst.at[r, pl.ds(pl.multiple_of(t * piece, piece), piece)],
-            send_sem=send_sem.at[r],
-            recv_sem=recv_sem.at[r],
-            device_id={"ta": dest},
-            device_id_type=MESH,
-        )
-
-    def send_all(src, dst, r, send_sem, recv_sem, skip_first):
-        for c, k in peers:
-            dest = peer(c, k)
-            if skip_first:
-
-                @pl.when(dest > 0)
-                def _():
-                    exchange(src, dst, r, dest, send_sem, recv_sem).start()
-
-            else:
-                exchange(src, dst, r, dest, send_sem, recv_sem).start()
-        own = pl.ds(pl.multiple_of(t * piece, piece), piece)
-        dst[r, own] = src[r, own]
-
-    def whole(src, dst, r, send_sem, recv_sem):
-        return pltpu.make_async_remote_copy(
-            src_ref=src.at[r, pl.ds(0, (n - 1) * piece)],
-            dst_ref=dst.at[r, pl.ds(0, (n - 1) * piece)],
-            send_sem=send_sem.at[r],
-            recv_sem=recv_sem.at[r],
-            device_id={"ta": lax.rem(t + 1, n)},
-            device_id_type=MESH,
-        )
-
-    def temporal_row(r):
-        @pl.when(t > 0)
-        def _():
-            hidden_copy(r).wait_recv()
-
-        lhs = jnp.concatenate(
-            [hv[r, 2 - k : 2 - k + frames].reshape(tokens, channels) for k in range(3)], axis=1
-        )
-        total = xv[r + 1].reshape(tokens, channels).astype(F32) + dot(lhs, wt[...])
-        rounded = total.astype(BF16)
-        mixed[r] = rounded
-        wide = rounded.astype(F32)
-        scale = lax.rsqrt(jnp.mean(wide * wide, axis=-1, keepdims=True) + 1e-06)
-        normed = (wide * scale * gv[...]).astype(BF16)
-        sv[r] = dot(perm[0], normed).astype(BF16)
-
     up = pltpu.make_async_remote_copy(
         src_ref=clip.at[:, 0],
         dst_ref=xv.at[rows + 1],
@@ -267,19 +167,193 @@
         def _():
             pl.semaphore_signal(late, inc=1, device_id={"ta": k}, device_id_type=MESH)
 
-    for load in clip_loads + space_loads:
+    row_i = lax.broadcasted_iota(jnp.int32, (tokens, tokens), 0)
+    col_i = lax.broadcasted_iota(jnp.int32, (tokens, tokens), 1)
+    clip_len = n * frames
+    natural = (
+        lax.rem(row_i // cols, frames) * width + (row_i // piece) * cols + lax.rem(row_i, cols)
+    )
+    perm[0] = jnp.where(natural == col_i, 1.0, 0.0).astype(BF16)
+    natural_t = (
+        lax.rem(col_i // cols, frames) * width + (col_i // piece) * cols + lax.rem(col_i, cols)
+    )
+    perm[1] = jnp.where(natural_t == row_i, 1.0, 0.0).astype(BF16)
+    by_col = lax.rem(row_i, clip_len) * cols + row_i // clip_len
+    perm[2] = jnp.where(by_col == col_i, 1.0, 0.0).astype(BF16)
+    by_col_t = lax.rem(col_i, clip_len) * cols + col_i // clip_len
+    perm[3] = jnp.where(by_col_t == row_i, 1.0, 0.0).astype(BF16)
+
+    @pl.when(g == 0)
+    def _():
+        xv[0] = jnp.zeros(xv.shape[1:], BF16)
+
+    @pl.when(g == ny - 1)
+    def _():
+        xv[rows + 1] = jnp.zeros(xv.shape[1:], BF16)
+
+    @pl.when(t == 0)
+    def _():
+        hv[:, 0:2] = jnp.zeros((rows, 2) + hv.shape[2:], BF16)
+
+    def conv_frames(r, first, count, arrived=lambda b: None):
+        these = count * width
+        column = lax.rem(lax.broadcasted_iota(jnp.int32, (these, channels), 0), width)
+        here = pl.ds(first, count)
+        lhs = jnp.concatenate(
+            [xv[r + a, here].reshape(these, channels) for a in range(3)], axis=1
+        )
+        arrived(0)
+        left = pltpu.roll(dot(lhs, ws[0]), 1, 0)
+        arrived(1)
+        total = jnp.where(column == 0, 0.0, left) + dot(lhs, ws[1])
+        arrived(2)
+        right = pltpu.roll(dot(lhs, ws[2]), these - 1, 0)
+        total = total + jnp.where(column == width - 1, 0.0, right)
+        hidden = (total * jax.nn.sigmoid(total)).astype(BF16)
+        hv[r, pl.ds(first + 2, count)] = hidden.reshape(count, width, channels)
+
+    def hidden_copy(r):
+        return pltpu.make_async_remote_copy(
+            src_ref=hv.at[r, pl.ds(frames, 2)],
+            dst_ref=hv.at[r, pl.ds(0, 2)],
+            send_sem=h_send.at[r],
+            recv_sem=h_recv.at[r],
+            device_id={"ta": lax.rem(t + 1, n)},
+            device_id_type=MESH,
+        )
+
+    def send_hidden(r):
+        @pl.when(t < n - 1)
+        def _():
+            hidden_copy(r).start()
+
+    def exchange(src, dst, r, dest, send_sem, recv_sem):
+        return pltpu.make_async_remote_copy(
+            src_ref=src.at[r, pl.ds(pl.multiple_of(dest * piece, piece), piece)],
+            dst_ref=dst.at[r, pl.ds(pl.multiple_of(t * piece, piece), piece)],
+            send_sem=send_sem.at[r],
+            recv_sem=recv_sem.at[r],
+            device_id={"ta": dest},
+            device_id_type=MESH,
+        )
+
+    def keep_own(src, dst, r):
+        own = pl.ds(pl.multiple_of(t * piece, piece), piece)
+        dst[r, own] = src[r, own]
+
+    def send_normed(r, i):
+        for c, k in peers:
+            dest = peer(c, k)
+
+            @pl.when((dest > 0) | (i > 0))
+            def _():
+                exchange(sv, rv, r, dest, a_send, a_recv).start()
+
+        keep_own(sv, rv, r)
+
+    step = half // 2
+
+    def to_relay(k):
+        dest = peer(half, k)
+        return pltpu.make_async_remote_copy(
+            src_ref=av.at[1, pl.ds(pl.multiple_of(dest * piece, piece), piece)],
+            dst_ref=passing.at[pl.ds(k * piece, piece)],
+            send_sem=b_send.at[1],
+            recv_sem=pass_recv,
+            device_id={"ta": peer(-step, 0)},
+            device_id_type=MESH,
+        )
+
+    def from_relay(k):
+        origin = peer(step, 0)
+        return pltpu.make_async_remote_copy(
+            src_ref=passing.at[pl.ds(k * piece, piece)],
+            dst_ref=ov.at[1, pl.ds(pl.multiple_of(origin * piece, piece), piece)],
+            send_sem=pass_send,
+            recv_sem=b_recv.at[1],
+            device_id={"ta": peer(-step, k)},
+            device_id_type=MESH,
+        )
+
+    def pass_whole():
+        return pltpu.make_async_remote_copy(
+            src_ref=passing,
+            dst_ref=passing,
+            send_sem=pass_send,
+            recv_sem=pass_recv,
+            device_id={"ta": peer(-step, 0)},
+            device_id_type=MESH,
+        )
+
+    def send_attended(r, i):
+        for c, k in peers:
+            if c == half:
+
+                @pl.when(i == 0)
+                def _():
+                    to_relay(k).start()
+
+                @pl.when(i > 0)
+                def _():
+                    exchange(av, ov, r, peer(c, k), b_send, b_recv).start()
+
+            else:
+                exchange(av, ov, r, peer(c, k), b_send, b_recv).start()
+        keep_own(av, ov, r)
+
+    def whole(src, dst, r, send_sem, recv_sem):
+        return pltpu.make_async_remote_copy(
+            src_ref=src.at[r, pl.ds(0, (n - 1) * piece)],
+            dst_ref=dst.at[r, pl.ds(0, (n - 1) * piece)],
+            send_sem=send_sem.at[r],
+            recv_sem=recv_sem.at[r],
+            device_id={"ta": lax.rem(t + 1, n)},
+            device_id_type=MESH,
+        )
+
+    def temporal_row(r):
+        @pl.when(t > 0)
+        def _():
+            hidden_copy(r).wait_recv()
+
+        lhs = jnp.concatenate(
+            [hv[r, 2 - k : 2 - k + frames].reshape(tokens, channels) for k in range(3)], axis=1
+        )
+        total = xv[r + 1].reshape(tokens, channels).astype(F32) + dot(lhs, wt[...])
+        rounded = total.astype(BF16)
+        mixed[r] = rounded
+        wide = rounded.astype(F32)
+        scale = lax.rsqrt(jnp.mean(wide * wide, axis=-1, keepdims=True) + 1e-06)
+        normed = (wide * scale * gv[...]).astype(BF16)
+        sv[r] = dot(perm[0], normed).astype(BF16)
+
+    def space_arrived(b):
+        for load in space_loads[3 * b : 3 * b + 3]:
+            load.wait()
+
+    for load in clip_loads:
         load.wait()
+    conv_frames(1, frames - 2, 2, space_arrived)
     for load in other_loads:
         load.start()
-    lax.fori_loop(1, rows - 1, lambda r, c: (conv_row(r), c)[1], 0)
 
     @pl.when((t > 0) & (t < n - 1))
     def _():
         pl.semaphore_wait(next_ready, 1)
 
-    for r in range(1, rows - 1):
+    send_hidden(1)
+
+    def inner_last(r, c):
+        conv_frames(r, frames - 2, 2)
         send_hidden(r)
-
+        return c
+
+    def inner_first(r, c):
+        conv_frames(r, 0, frames - 2)
+        return c
+
+    lax.fori_loop(2, rows - 1, inner_last, 0)
+    lax.fori_loop(1, rows - 1, inner_first, 0)
     for load in other_loads:
         load.wait()
 
@@ -294,10 +368,15 @@
         def _():
             pl.semaphore_wait(ready, n - 1 - t)
 
-        send_all(sv, rv, r, a_send, a_recv, True)
+        @pl.when((i == 1) & (t > 0))
+        def _():
+            pl.semaphore_wait(late, 1)
+            exchange(sv, rv, order(0), 0, a_send, a_recv).start()
+
+        send_normed(r, i)
         return c
 
-    before = jnp.where((t == 0) | (t >= n // 2), 1, 0)
+    before = jnp.where((t == 0) | (t >= early), 1, 0)
     lax.fori_loop(0, before, temporal, 0)
 
     @pl.when(g > 0)
@@ -310,18 +389,12 @@
 
     def edge(i, c):
         r = i * (rows - 1)
-        conv_row(r)
+        conv_frames(r, 0, frames)
         send_hidden(r)
         return c
 
     lax.fori_loop(0, 2, edge, 0)
     lax.fori_loop(before, rows, temporal, 0)
-
-    @pl.when(t > 0)
-    def _():
-        pl.semaphore_wait(late, 1)
-        for r in list(range(1, rows - 1)) + [0, rows - 1]:
-            exchange(sv, rv, r, 0, a_send, a_recv).start()
 
     head_dim = channels // HEADS
     quad = 4 * head_dim
@@ -362,13 +435,16 @@
             total = dot(expo[:, four], ones[...])
             att[:, four] = (summed[:, four] / total).astype(BF16)
         av[r] = dot(perm[3], att[...]).astype(BF16)
-        send_all(av, ov, r, b_send, b_recv, False)
+        send_attended(r, i)
         return carry
 
     lax.fori_loop(0, rows, attend_row, 0)
+    pass_whole().wait_recv()
+    for k in range(2):
+        from_relay(k).start()
 
     def out_row(i, carry):
-        r = order(i)
+        r = order(lax.rem(i + 1, rows))
         whole(av, ov, r, b_send, b_recv).wait_recv()
         attended = dot(perm[1], ov[r]).astype(BF16)
         total = mixed[r].astype(F32) + dot(attended, wo[...])
@@ -376,6 +452,8 @@
         return carry
 
     lax.fori_loop(0, rows, out_row, 0)
+
+    pass_whole().wait_send()
 
     @pl.when(g > 0)
     def _():
@@ -442,6 +520,9 @@
                 pltpu.SemaphoreType.REGULAR,
                 pltpu.SemaphoreType.REGULAR,
                 pltpu.SemaphoreType.REGULAR,
+                pltpu.VMEM((2 * frames * (width // n), channels), BF16),
+                dma,
+                dma,
             ],
             compiler_params=pltpu.CompilerParams(
                 collective_id=0, has_side_effects=True, vmem_limit_bytes=48 * 2**20

time: 70.5 us -> 68.5 us (0.972)
  Pallas kernels: 69.4 us -> 67.1 us
    pallas_call x1, Pallas kernels: 69.4 us -> 67.1 us  [per_device(): pl.pallas_call(functools.partial(block_kernel, n, ny), out_shape=pltpu.VM...]
where the time goes in v4:
time: 68.5 us; the launch traced here: 68.1 us
  Pallas kernels  67.1 us (98%)
  local copies, waits for them, and re-layouts  0.97 us (1%)
    pallas_call x1, Pallas kernels, per_device(): pl.pallas_call(functools.partial(block_kernel, n, ny), out_shape=pltpu.VM...  67.1 us

profile of v4, /device:TPU:513, one launch (start us, length us, event | category | flops | bytes accessed | tf_op | source)
XLA Modules:
  0.0 68.1 jit_solution(5199086194214237846)
XLA Ops:
  0.0 67.1 %shard_map.64 = bf16[4,4,64,512]{3,2,1,0:T(8,128)(2,1)S(1)} custom-call(bf16[4,4,64,512]{3,2,1,0:T(8,128)(2,1)} %clip.1, bf16[3,3,512,512]{3,2,1,0:T(8,128)(2,1)} %w_space.1, bf16[1536,512]{1,0:T(8,128)(2,1)} %bitcast.2, bf16[512,1536]{1,0:T(8,128)(2,1)} %w_qkv.1, bf16[512,512]{1,0:T(8,128)(2,1)} %w_out.1, f32[1,512]{1,0:T(1,128)} %bitcast.3), custom_call_target="tpu_custom_call" | custom-call | tf_op jit(solution)/shard_map/pallas_call | solution.py:484
  67.1 1.0 %copy.8 = bf16[4,4,64,512]{3,2,1,0:T(8,128)(2,1)} copy(bf16[4,4,64,512]{3,2,1,0:T(8,128)(2,1)S(1)} %shard_map.64) | data formatting | bytes 2097152

commit v5 on v4

--- a/solution.py
+++ b/solution.py
@@ -435,16 +435,19 @@
             total = dot(expo[:, four], ones[...])
             att[:, four] = (summed[:, four] / total).astype(BF16)
         av[r] = dot(perm[3], att[...]).astype(BF16)
+        @pl.when(i == rows - 1)
+        def _():
+            pass_whole().wait_recv()
+            for k in range(2):
+                from_relay(k).start()
+
         send_attended(r, i)
         return carry
 
     lax.fori_loop(0, rows, attend_row, 0)
-    pass_whole().wait_recv()
-    for k in range(2):
-        from_relay(k).start()
 
     def out_row(i, carry):
-        r = order(lax.rem(i + 1, rows))
+        r = order(jnp.where(i < rows - 1, lax.rem(i + 1, rows - 1), rows - 1))
         whole(av, ov, r, b_send, b_recv).wait_recv()
         attended = dot(perm[1], ov[r]).astype(BF16)
         total = mixed[r].astype(F32) + dot(attended, wo[...])

time: 68.5 us -> 68.2 us (level)
  no operation moved by 1% of the time
where the time goes in v5:
time: 68.2 us; the launch traced here: 68.1 us
  Pallas kernels  67.1 us (98%)
  local copies, waits for them, and re-layouts  0.97 us (1%)
    pallas_call x1, Pallas kernels, per_device(): pl.pallas_call(functools.partial(block_kernel, n, ny), out_shape=pltpu.VM...  67.1 us

profile of v5, /device:TPU:513, one launch (start us, length us, event | category | flops | bytes accessed | tf_op | source)
XLA Modules:
  0.0 68.1 jit_solution(13056292823869150620)
XLA Ops:
  0.0 67.1 %shard_map.64 = bf16[4,4,64,512]{3,2,1,0:T(8,128)(2,1)S(1)} custom-call(bf16[4,4,64,512]{3,2,1,0:T(8,128)(2,1)} %clip.1, bf16[3,3,512,512]{3,2,1,0:T(8,128)(2,1)} %w_space.1, bf16[1536,512]{1,0:T(8,128)(2,1)} %bitcast.2, bf16[512,1536]{1,0:T(8,128)(2,1)} %w_qkv.1, bf16[512,512]{1,0:T(8,128)(2,1)} %w_out.1, f32[1,512]{1,0:T(1,128)} %bitcast.3), custom_call_target="tpu_custom_call" | custom-call | tf_op jit(solution)/shard_map/pallas_call | solution.py:487
  67.1 1.0 %copy.8 = bf16[4,4,64,512]{3,2,1,0:T(8,128)(2,1)} copy(bf16[4,4,64,512]{3,2,1,0:T(8,128)(2,1)S(1)} %shard_map.64) | data formatting | bytes 2097152
